TPU v7x, 32 devices: a whole 2x2x4 slice. The times are simulated.
32 devices in a mesh: expert: 4 (over z), tensor: 8 (over y, x, core).
Axes of the slice: x: 2, y: 2, z: 4, core: 2. Of those that a mesh axis runs over, the one named last changes fastest.
Arguments:
- stashed: bfloat16 [384, 4096], P('expert', 'tensor'), may hold values from -6 to 6
- expert_ids: int32 [384, 2], P('expert'), may hold values from 0 to 3, all different within a row; in each aligned block of 96 rows (0 to 95, 96 to 191, ...) at most 64 rows name the same one
- combine_weight: float32 [384, 2], P('expert'), may hold values from 0.2 to 1
- w_gate: bfloat16 [4, 7168, 4096], P('expert', 'tensor'), may hold values from -0.09375 to 0.09375
- w_up: bfloat16 [4, 7168, 4096], P('expert', 'tensor'), may hold values from -0.09375 to 0.09375
- w_down: bfloat16 [4, 7168, 4096], P('expert', 'tensor'), may hold values from -0.09375 to 0.09375
Outputs:
- mixed_out: bfloat16 [384, 4096], P('expert', 'tensor')
Inputs may be any that keep to these rules, and one draw needn't show every extreme that they name: `expert_ids`: each row names two different experts. Among the 96 rows of one group (aligned blocks) no expert is named more than 64 times, and in some group some expert is named exactly 64 times.
All inputs are finite; a program needn't handle non-finite values.
Results may differ from a plain program's by a relative error of at most 0.0049.
Values may be sent and summed in bfloat16 or wider, within the bound.
A program may use at most 64 MiB of HBM per device.

v0:
```python
import functools

import jax
import jax.numpy as jnp
from jax import lax
from jax.experimental import pallas as pl
from jax.experimental.pallas import tpu as pltpu
from jax.sharding import PartitionSpec as P


def slot_targets(expert_ids, experts, capacity):
    flat_ids = expert_ids.reshape(-1)
    one_hot = (flat_ids[:, None] == jnp.arange(experts, dtype=jnp.int32)[None, :]).astype(jnp.int32)
    before = jnp.cumsum(one_hot, axis=0) - one_hot
    slot_index = jnp.sum(before * one_hot, axis=1)
    return (flat_ids * capacity + slot_index).reshape(expert_ids.shape)


def contract_last(left, right):
    return lax.dot_general(
        left, right, (((1,), (1,)), ((), ())), preferred_element_type=jnp.float32
    )


def contract_first(left, right):
    return lax.dot_general(
        left, right, (((0,), (0,)), ((), ())), preferred_element_type=jnp.float32
    )


def shards(stashed, expert_ids, combine_weight, w_gate, w_up, w_down):
    tok_count = stashed.shape[0]
    feat_width = stashed.shape[1]
    experts = lax.axis_size("expert")
    capacity = min(tok_count, 8 * tok_count // (3 * experts))
    targets = slot_targets(expert_ids, experts, capacity)
    columns = jnp.arange(experts * capacity, dtype=jnp.int32)
    pair_match = (targets[:, :, None] == columns[None, None, :]).astype(jnp.float32)
    selector = jnp.sum(pair_match, axis=1).T.astype(jnp.bfloat16)
    mixing = jnp.sum(pair_match * combine_weight[:, :, None], axis=1)
    gate_w = w_gate[0]
    up_w = w_up[0]
    down_w = w_down[0]
    gathered = lax.all_gather(stashed, "tensor", axis=1, tiled=True)
    outgoing = jnp.dot(selector, gathered, preferred_element_type=jnp.float32).astype(jnp.bfloat16)
    outgoing = outgoing.reshape(experts, capacity, gathered.shape[1])
    received = lax.all_to_all(outgoing, "expert", split_axis=0, concat_axis=0, tiled=True)
    sources, item_count, full_width = received.shape
    rows_in = received.reshape(sources * item_count, full_width)
    gate_acts = contract_last(rows_in, gate_w)
    up_acts = contract_last(rows_in, up_w)
    hidden = (jax.nn.silu(gate_acts) * up_acts).astype(jnp.bfloat16)
    result = jnp.dot(hidden, down_w, preferred_element_type=jnp.float32)
    partial_value = result.reshape(sources, item_count, result.shape[1])
    partial_value = partial_value.reshape(-1, partial_value.shape[2])
    own_share = lax.psum_scatter(partial_value, "tensor", scatter_dimension=1, tiled=True)
    returned_rows = lax.all_to_all(
        own_share.reshape(experts, capacity, feat_width),
        "expert",
        split_axis=0,
        concat_axis=0,
        tiled=True,
    )
    combined = jnp.dot(
        mixing,
        returned_rows.reshape(experts * capacity, feat_width),
        precision=lax.Precision.HIGHEST,
        preferred_element_type=jnp.float32,
    )
    return combined.astype(jnp.bfloat16)


MESH = pl.DeviceIdType.MESH


def flip(index, bit):
    return index + bit - 2 * bit * lax.rem(lax.div(index, bit), 2)


def layer_kernel(
    groups, cap,
    x_ref, ids_ref, cw_ref, wg_hbm, wu_hbm, wd_hbm, out_ref,
    wg, wu, wd, picked, rows_in, gate_acc, up_acc, hidden,
    sib_out, sib_in, own_part, d_out, d_in, x_out, x_in, y_out, y_in, z_out, z_in,
    w_sem, send_sem, recv_sem,
):
    tokens, feat = x_ref.shape
    z = lax.axis_index("expert")
    t = lax.axis_index("tensor")
    sib, tx, ty = flip(t, 1), flip(t, 2), flip(t, 4)
    td = flip(tx, 4)
    group_of = [z, flip(z, 1), flip(z, 2), flip(flip(z, 1), 2)]
    steps = range(groups)

    loads = []
    for i, (hbm, vmem) in enumerate(((wg_hbm, wg), (wu_hbm, wu), (wd_hbm, wd))):
        half = vmem.shape[0] // 2
        for j in range(2):
            part = pl.ds(j * half, half)
            loads.append(pltpu.make_async_copy(hbm.at[0, part], vmem.at[part], w_sem.at[2 * i + j]))
    for load in loads:
        load.start()

    barrier = pltpu.get_barrier_semaphore()
    peers = [{"tensor": sib}, {"tensor": tx}, {"tensor": ty}]
    peers += [{"expert": group_of[s]} for s in steps[1:]]
    for peer in peers:
        pl.semaphore_signal(barrier, inc=1, device_id=peer, device_id_type=MESH)

    ids = ids_ref[...]
    experts_at = lax.broadcasted_iota(jnp.int32, (8, tokens), 0)
    first = (ids[0:1] == experts_at).astype(jnp.float32)
    second = (ids[1:2] == experts_at).astype(jnp.float32)
    earlier = (
        lax.broadcasted_iota(jnp.int32, (tokens, tokens), 0)
        < lax.broadcasted_iota(jnp.int32, (tokens, tokens), 1)
    ).astype(jnp.bfloat16)
    before = jnp.dot((first + second).astype(jnp.bfloat16), earlier, preferred_element_type=jnp.float32)
    slot0 = jnp.sum(before * first, axis=0, keepdims=True)
    slot1 = jnp.sum((before + first) * second, axis=0, keepdims=True)
    place = (ids ^ z).astype(jnp.float32) * cap
    slots = lax.broadcasted_iota(jnp.int32, (groups * cap, tokens), 0).astype(jnp.float32)
    match0 = (slots == place[0:1] + slot0).astype(jnp.float32)
    match1 = (slots == place[1:2] + slot1).astype(jnp.float32)
    selector = (match0 + match1).astype(jnp.bfloat16)
    picked[...] = jnp.dot(selector, x_ref[...], preferred_element_type=jnp.float32).astype(jnp.bfloat16)

    def group_rows(s):
        return pl.ds(pl.multiple_of(group_of[s] * cap, cap), cap)

    def block(owner, s):
        lanes_at = pl.ds(pl.multiple_of(lax.rem(owner, 2) * feat, feat), feat)
        return rows_in.at[lax.div(owner, 2), group_rows(s), lanes_at]

    copies = {}

    def send(name, s, src, dst, peer):
        number = NAMES.index(name) * groups + s
        copy = pltpu.make_async_remote_copy(
            src_ref=src, dst_ref=dst, send_sem=send_sem.at[number], recv_sem=recv_sem.at[number],
            device_id=peer, device_id_type=MESH,
        )
        copy.start()
        copies[name, s] = copy

    def arrive(name, s):
        copies[name, s].wait_recv()

    own_at = block(t, 0)
    own_at[...] = picked[pl.ds(0, cap)]
    pl.semaphore_wait(barrier, len(peers))

    def share(s):
        here = block(t, s)
        send("own_x", s, here, here, {"tensor": tx})
        send("own_y", s, here, here, {"tensor": ty})
        send("own_sib", s, here, here, {"tensor": sib})

    def pass_x(s):
        arrive("own_x", s)
        here = block(tx, s)
        if s % 2 == 0:
            send("diag", s, here, here, {"tensor": ty})
        send("sib_x", s, here, here, {"tensor": sib})

    def pass_y(s):
        arrive("own_y", s)
        here = block(ty, s)
        if s % 2 == 1:
            send("diag", s, here, here, {"tensor": tx})
        send("sib_y", s, here, here, {"tensor": sib})

    def pass_diag(s):
        arrive("diag", s)
        here = block(td, s)
        send("sib_d", s, here, here, {"tensor": sib})

    def project(owner, start):
        pair = lax.div(owner, 2)
        rows = rows_in[pair]
        lanes_at = pl.ds(pl.multiple_of(pair * (2 * feat), 2 * feat), 2 * feat)
        for weight, acc in ((wg, gate_acc), (wu, up_acc)):
            part = contract_last(rows, weight[:, lanes_at])
            acc[...] = part if start else acc[...] + part

    for s in (1, 2, 3):
        send("z", s, picked.at[pl.ds(s * cap, cap)], block(t, 0), {"expert": group_of[s]})
    share(0)
    arrive("z", 1)
    share(1)
    pass_x(0)
    pass_y(0)
    pass_x(1)
    pass_y(1)
    arrive("z", 2)
    share(2)
    arrive("z", 3)
    share(3)
    pass_diag(0)
    pass_diag(1)
    for load in loads[:4]:
        load.wait()
    for s in steps:
        arrive("own_sib", s)
    project(t, True)
    pass_x(2)
    pass_y(2)
    pass_x(3)
    pass_y(3)
    for s in steps:
        arrive("sib_x", s)
    project(tx, False)
    pass_diag(2)
    pass_diag(3)
    for s in steps:
        arrive("sib_y", s)
    project(ty, False)
    for s in steps:
        arrive("sib_d", s)
    project(td, False)
    gate = gate_acc[...]
    hidden[...] = (gate / (1.0 + jnp.exp(-gate)) * up_acc[...]).astype(jnp.bfloat16)
    for load in loads[4:]:
        load.wait()

    owners = (t, tx, ty, td)

    def down(owner):
        lanes_at = pl.ds(pl.multiple_of(owner * feat, feat), feat)
        return jnp.dot(hidden[...], wd[:, lanes_at], preferred_element_type=jnp.float32)

    def partial_sums(q):
        sib_out[q] = down(flip(owners[q], 1)).astype(jnp.bfloat16)
        send("sum_sib", q, sib_out.at[q], sib_in.at[q], {"tensor": sib})
        own_part[q] = down(owners[q])

    def chip_sum(q, s):
        at = group_rows(s)
        return own_part[q, at] + sib_in[q, at].astype(jnp.float32)

    def sum_d(s):
        d_out[s] = chip_sum(3, s).astype(jnp.bfloat16)
        send("sum_d", s, d_out.at[s], d_in.at[s], {"tensor": tx if s % 2 == 0 else ty})

    def sum_x(s):
        value = chip_sum(1, s)
        if s % 2 == 1:
            arrive("sum_d", s)
            value = value + d_in[s].astype(jnp.float32)
        x_out[s] = value.astype(jnp.bfloat16)
        send("sum_x", s, x_out.at[s], x_in.at[s], {"tensor": tx})

    def sum_y(s):
        value = chip_sum(2, s)
        if s % 2 == 0:
            arrive("sum_d", s)
            value = value + d_in[s].astype(jnp.float32)
        y_out[s] = value.astype(jnp.bfloat16)
        send("sum_y", s, y_out.at[s], y_in.at[s], {"tensor": ty})

    def total(s):
        arrive("sum_x", s)
        arrive("sum_y", s)
        value = chip_sum(0, s) + x_in[s].astype(jnp.float32) + y_in[s].astype(jnp.float32)
        return value.astype(jnp.bfloat16)

    def give_back(s):
        z_out[s] = total(s)
        send("back", s, z_out.at[s], z_in.at[pl.ds(s * cap, cap)], {"expert": group_of[s]})

    partial_sums(3)
    partial_sums(1)
    arrive("sum_sib", 3)
    sum_d(2)
    sum_d(3)
    partial_sums(2)
    arrive("sum_sib", 1)
    sum_x(2)
    arrive("sum_sib", 2)
    sum_y(3)
    sum_d(0)
    sum_d(1)
    partial_sums(0)
    sum_x(3)
    sum_y(2)
    sum_x(0)
    sum_y(1)
    arrive("sum_sib", 0)
    sum_x(1)
    sum_y(0)
    give_back(2)
    give_back(3)
    give_back(1)
    z_in[pl.ds(0, cap)] = total(0)

    weights = cw_ref[...]
    mixing = match0 * weights[0:1] + match1 * weights[1:2]
    coarse = mixing.astype(jnp.bfloat16)
    fine = (mixing - coarse.astype(jnp.float32)).astype(jnp.bfloat16)
    for s in (2, 3, 1):
        arrive("back", s)
    returned = z_in[...]
    combined = contract_first(coarse, returned) + contract_first(fine, returned)
    out_ref[...] = combined.astype(jnp.bfloat16)
    for copy in copies.values():
        copy.wait_send()


NAMES = (
    "z", "own_x", "own_y", "own_sib", "diag", "sib_x", "sib_y", "sib_d",
    "sum_sib", "sum_d", "sum_x", "sum_y", "back",
)


def fused_shards(stashed, expert_ids, combine_weight, w_gate, w_up, w_down):
    groups = lax.axis_size("expert")
    tokens, feat = stashed.shape
    cap = min(tokens, 8 * tokens // (3 * groups))
    _, units, width = w_gate.shape
    rows = groups * cap
    bf16, f32 = jnp.bfloat16, jnp.float32
    vmem = pl.BlockSpec(memory_space=pltpu.VMEM)
    hbm = pl.BlockSpec(memory_space=pl.ANY)
    pieces = [pltpu.VMEM((groups, cap, feat), bf16)] * 7
    return pl.pallas_call(
        functools.partial(layer_kernel, groups, cap),
        out_shape=jax.ShapeDtypeStruct((tokens, feat), bf16),
        in_specs=[vmem, vmem, vmem, hbm, hbm, hbm],
        out_specs=vmem,
        scratch_shapes=[
            pltpu.VMEM((units, width), bf16),
            pltpu.VMEM((units, width), bf16),
            pltpu.VMEM((units, width), bf16),
            pltpu.VMEM((rows, feat), bf16),
            pltpu.VMEM((width // (2 * feat), rows, 2 * feat), bf16),
            pltpu.VMEM((rows, units), f32),
            pltpu.VMEM((rows, units), f32),
            pltpu.VMEM((rows, units), bf16),
            pltpu.VMEM((4, rows, feat), bf16),
            pltpu.VMEM((4, rows, feat), bf16),
            pltpu.VMEM((4, rows, feat), f32),
            *pieces,
            pltpu.VMEM((rows, feat), bf16),
            pltpu.SemaphoreType.DMA((6,)),
            pltpu.SemaphoreType.DMA((len(NAMES) * groups,)),
            pltpu.SemaphoreType.DMA((len(NAMES) * groups,)),
        ],
        compiler_params=pltpu.CompilerParams(
            collective_id=0, has_side_effects=True, vmem_limit_bytes=60 * 1024 * 1024
        ),
    )(stashed, expert_ids.T, combine_weight.T, w_gate, w_up, w_down)


def picks_kernel(mesh):
    return mesh.shape["tensor"] == 8 and mesh.shape["expert"] == 4


def solution(mesh):
    return jax.shard_map(
        fused_shards if picks_kernel(mesh) else shards,
        mesh=mesh,
        in_specs=(
            P("expert", "tensor"),
            P("expert", None),
            P("expert", None),
            P("expert", "tensor", None),
            P("expert", "tensor", None),
            P("expert", "tensor", None),
        ),
        out_specs=P("expert", "tensor"),
        check_vma=False,
    )
```

profile of v0, /device:TPU:0, one launch (start us, length us, event | category | flops | bytes accessed | tf_op | source)
XLA Modules:
  0.0 44.9 jit_solution(9271362369926806738)
XLA Ops:
  0.0 43.4 %shard_map.64 = bf16[96,512]{1,0:T(8,128)(2,1)} custom-call(bf16[96,512]{1,0:T(8,128)(2,1)} %x_ref.1, s32[2,96]{1,0:T(2,128)} %bitcast.2, f32[2,96]{1,0:T(2,128)} %bitcast.3, bf16[1,896,4096]{2,1,0:T(8,128)(2,1)} %wg_hbm.1, bf16[1,896,4096]{2,1,0:T(8,128)(2,1)} %wu_hbm.1, bf16[1,896,4096]{2,1,0:T(8,128)(2,1)} %wd_hbm.1), custom_call_target="tpu_custom_call" | custom-call | tf_op jit(solution)/shard_map/pallas_call | solution.py:325
  43.4 1.5 %copy.8 = bf16[96,512]{1,0:T(8,128)(2,1)} copy(bf16[96,512]{1,0:T(8,128)(2,1)} %shard_map.64) | data formatting | bytes 196608
where the time goes:
time: 45.1 us; the launch traced here: 44.9 us
  Pallas kernels  43.4 us (96%)
  local copies, waits for them, and re-layouts  1.54 us (3%)
    pallas_call x1, Pallas kernels, fused_shards(): pl.pallas_call(functools.partial(layer_kernel, groups, cap), out_shape=ja...  43.4 us
    unnamed x1, local copies, waits for them, and re-layouts  1.54 us

commit v1 on v0

v1 whole, which is shorter than its diff:
```python
import functools
import math

import jax
import jax.numpy as jnp
from jax import lax
from jax.experimental import pallas as pl
from jax.experimental.pallas import tpu as pltpu
from jax.sharding import PartitionSpec as P


def slot_targets(expert_ids, experts, capacity):
    flat_ids = expert_ids.reshape(-1)
    one_hot = (flat_ids[:, None] == jnp.arange(experts, dtype=jnp.int32)[None, :]).astype(jnp.int32)
    before = jnp.cumsum(one_hot, axis=0) - one_hot
    slot_index = jnp.sum(before * one_hot, axis=1)
    return (flat_ids * capacity + slot_index).reshape(expert_ids.shape)


def contract_last(left, right):
    return lax.dot_general(
        left, right, (((1,), (1,)), ((), ())), preferred_element_type=jnp.float32
    )


def contract_first(left, right):
    return lax.dot_general(
        left, right, (((0,), (0,)), ((), ())), preferred_element_type=jnp.float32
    )


def shards(stashed, expert_ids, combine_weight, w_gate, w_up, w_down):
    tok_count = stashed.shape[0]
    feat_width = stashed.shape[1]
    experts = lax.axis_size("expert")
    capacity = min(tok_count, 8 * tok_count // (3 * experts))
    targets = slot_targets(expert_ids, experts, capacity)
    columns = jnp.arange(experts * capacity, dtype=jnp.int32)
    pair_match = (targets[:, :, None] == columns[None, None, :]).astype(jnp.float32)
    selector = jnp.sum(pair_match, axis=1).T.astype(jnp.bfloat16)
    mixing = jnp.sum(pair_match * combine_weight[:, :, None], axis=1)
    gate_w = w_gate[0]
    up_w = w_up[0]
    down_w = w_down[0]
    gathered = lax.all_gather(stashed, "tensor", axis=1, tiled=True)
    outgoing = jnp.dot(selector, gathered, preferred_element_type=jnp.float32).astype(jnp.bfloat16)
    outgoing = outgoing.reshape(experts, capacity, gathered.shape[1])
    received = lax.all_to_all(outgoing, "expert", split_axis=0, concat_axis=0, tiled=True)
    sources, item_count, full_width = received.shape
    rows_in = received.reshape(sources * item_count, full_width)
    gate_acts = contract_last(rows_in, gate_w)
    up_acts = contract_last(rows_in, up_w)
    hidden = (jax.nn.silu(gate_acts) * up_acts).astype(jnp.bfloat16)
    result = jnp.dot(hidden, down_w, preferred_element_type=jnp.float32)
    partial_value = result.reshape(sources, item_count, result.shape[1])
    partial_value = partial_value.reshape(-1, partial_value.shape[2])
    own_share = lax.psum_scatter(partial_value, "tensor", scatter_dimension=1, tiled=True)
    returned_rows = lax.all_to_all(
        own_share.reshape(experts, capacity, feat_width),
        "expert",
        split_axis=0,
        concat_axis=0,
        tiled=True,
    )
    combined = jnp.dot(
        mixing,
        returned_rows.reshape(experts * capacity, feat_width),
        precision=lax.Precision.HIGHEST,
        preferred_element_type=jnp.float32,
    )
    return combined.astype(jnp.bfloat16)


MESH = pl.DeviceIdType.MESH


def flip(index, bit):
    return index + bit - 2 * bit * lax.rem(lax.div(index, bit), 2)


def layer_kernel(
    groups, cap,
    x_hbm, ids_hbm, cw_hbm, wg_hbm, wu_hbm, wd_hbm, out_ref,
    x_ref, ids_ref, cw_ref, wg, wu, wd, picked, rows_in, gate_acc, up_acc, hidden,
    sib_out, sib_in, own_part, d_out, d_in, x_out, y_out, xy_in, z_out, z_in,
    in_sem, w_sem, send_sem, recv_sem,
):
    tokens, feat = x_ref.shape
    part = feat // 2
    z = lax.axis_index("expert")
    t = lax.axis_index("tensor")
    core = lax.rem(t, 2)
    sib, tx, ty = flip(t, 1), flip(t, 2), flip(t, 4)
    td = flip(tx, 4)
    chip_of = [lax.div(owner, 2) for owner in (t, tx, ty, td)]
    group_of = [z, flip(z, 1), flip(z, 2), flip(flip(z, 1), 2)]
    steps, halves = range(groups), range(2)

    barrier = pltpu.get_barrier_semaphore()
    peers = [{"expert": group_of[s]} for s in steps[1:]]
    peers += [{"tensor": tx}, {"tensor": ty}, {"tensor": td}, {"tensor": sib}]
    for peer in peers:
        pl.semaphore_signal(barrier, inc=1, device_id=peer, device_id_type=MESH)

    inputs = []
    for i, (hbm, vmem) in enumerate(((ids_hbm, ids_ref), (x_hbm, x_ref), (cw_hbm, cw_ref))):
        inputs.append(pltpu.make_async_copy(hbm, vmem, in_sem.at[i]))
    loads = []
    for i, (hbm, vmem) in enumerate(((wg_hbm, wg), (wu_hbm, wu), (wd_hbm, wd))):
        half = vmem.shape[0] // 2
        for j in halves:
            at = pl.ds(j * half, half)
            loads.append(pltpu.make_async_copy(hbm.at[0, at], vmem.at[at], w_sem.at[i]))
    for load in inputs:
        load.start()

    earlier = (
        lax.broadcasted_iota(jnp.int32, (tokens, tokens), 0)
        < lax.broadcasted_iota(jnp.int32, (tokens, tokens), 1)
    ).astype(jnp.bfloat16)
    experts_at = lax.broadcasted_iota(jnp.int32, (8, tokens), 0)
    slots = lax.broadcasted_iota(jnp.int32, (groups * cap, tokens), 0).astype(jnp.float32)
    inputs[0].wait()
    ids = ids_ref[...]
    first = (ids[0:1] == experts_at).astype(jnp.float32)
    second = (ids[1:2] == experts_at).astype(jnp.float32)
    before = jnp.dot((first + second).astype(jnp.bfloat16), earlier, preferred_element_type=jnp.float32)
    slot0 = jnp.sum(before * first, axis=0, keepdims=True)
    slot1 = jnp.sum((before + first) * second, axis=0, keepdims=True)
    place = (ids ^ z).astype(jnp.float32) * cap
    match0 = (slots == place[0:1] + slot0).astype(jnp.float32)
    match1 = (slots == place[1:2] + slot1).astype(jnp.float32)
    selector = (match0 + match1).astype(jnp.bfloat16)
    inputs[1].wait()
    for load in loads:
        load.start()
    chosen = jnp.dot(selector, x_ref[...], preferred_element_type=jnp.float32).astype(jnp.bfloat16)
    for h in halves:
        lanes = slice(h * part, (h + 1) * part)
        picked[h] = chosen[cap:, lanes]
        rows_in[0, h, 0, 0:cap] = chosen[:cap, lanes]

    numbers, sent = {}, []
    straight = ()
    straight_back = ()

    def remote(key, src, dst, peer):
        number = numbers.setdefault(key, len(numbers))
        return pltpu.make_async_remote_copy(
            src_ref=src, dst_ref=dst, send_sem=send_sem.at[0], recv_sem=recv_sem.at[number],
            device_id=peer, device_id_type=MESH,
        )

    def send(key, src, dst, peer):
        sent.append(math.prod(src.shape))
        remote(key, src, dst, peer).start()

    def arrive(key, dst):
        remote(key, dst, dst, {"tensor": sib}).wait_recv()

    def wait_load(hbm, vmem, i):
        pltpu.make_async_copy(hbm.at[0], vmem, w_sem.at[i]).wait()

    def rows_of(s):
        return pl.ds(s * cap, cap)

    def block(q, h, r, s):
        return rows_in.at[q, h, r, rows_of(s)]

    def send_z(s, h):
        send(("z", s, h), picked.at[h, rows_of(s - 1)], block(0, h, 0, s), {"expert": group_of[s]})

    def own(s, h):
        here = block(0, h, 0, s)
        if s > 0:
            arrive(("z", s, h), here)
        send(("x", s, h), here, block(1, h, 0, s), {"tensor": tx})
        send(("y", s, h), here, block(2, h, 0, s), {"tensor": ty})
        send(("s", 0, h), here, block(0, h, 1, s), {"tensor": sib})

    def far(s, h):
        send(("d", s, h), block(0, h, 0, s), block(3, h, 0, s), {"tensor": td})

    def pass_x(s, h):
        here = block(1, h, 0, s)
        arrive(("x", s, h), here)
        if (s + h) % 2 == 0 and (s, h) not in straight:
            send(("d", s, h), here, block(3, h, 0, s), {"tensor": ty})
        send(("s", 1, h), here, block(1, h, 1, s), {"tensor": sib})

    def pass_y(s, h):
        here = block(2, h, 0, s)
        arrive(("y", s, h), here)
        if (s + h) % 2 == 1 and (s, h) not in straight:
            send(("d", s, h), here, block(3, h, 0, s), {"tensor": tx})
        send(("s", 2, h), here, block(2, h, 1, s), {"tensor": sib})

    def pass_d(s, h):
        here = block(3, h, 0, s)
        arrive(("d", s, h), here)
        send(("s", 3, h), here, block(3, h, 1, s), {"tensor": sib})

    started = []

    def project(q, h):
        arrive(("s", q, h), rows_in.at[q, h, 1])
        for weight, acc in ((wg, gate_acc), (wu, up_acc)):
            value = None if not started else acc[...]
            for r in range(2):
                at = chip_of[q] * (2 * feat) + (core ^ r) * feat + h * part
                lanes = pl.ds(pl.multiple_of(at, part), part)
                term = contract_last(rows_in[q, h, r], weight[:, lanes])
                value = term if value is None else value + term
            acc[...] = value
        started.append(q)

    pl.semaphore_wait(barrier, len(peers))
    for s, h in ((1, 0), (1, 1), (2, 0), (3, 0), (2, 1), (3, 1)): send_z(s, h)
    own(0, 0)
    own(0, 1)
    pass_x(0, 0)
    pass_y(0, 0)
    own(1, 0)
    pass_x(0, 1)
    pass_y(0, 1)
    own(1, 1)
    own(2, 0)
    own(3, 0)
    pass_x(1, 0)
    pass_y(1, 0)
    pass_x(1, 1)
    pass_y(1, 1)
    pass_d(0, 0)
    pass_d(0, 1)
    wait_load(wg_hbm, wg, 0)
    wait_load(wu_hbm, wu, 1)
    project(0, 0)
    pass_x(2, 0)
    pass_y(2, 0)
    pass_x(3, 0)
    pass_y(3, 0)
    own(2, 1)
    own(3, 1)
    pass_d(1, 0)
    pass_d(1, 1)
    project(0, 1)
    project(1, 0)
    pass_x(2, 1)
    pass_y(2, 1)
    project(2, 0)
    pass_x(3, 1)
    pass_y(3, 1)
    pass_d(2, 0)
    pass_d(3, 0)
    project(3, 0)
    project(1, 1)
    pass_d(2, 1)
    pass_d(3, 1)
    project(2, 1)
    project(3, 1)

    wide = 2 * feat
    half_rows = groups * cap // 2

    def activate(j):
        at = pl.ds(j * half_rows, half_rows)
        gate = gate_acc[at]
        hidden[at] = (gate / (1.0 + jnp.exp(-gate)) * up_acc[at]).astype(jnp.bfloat16)

    def down(q, j):
        at = pl.ds(j * half_rows, half_rows)
        lanes = pl.ds(pl.multiple_of(chip_of[q] * wide, wide), wide)
        value = jnp.dot(hidden[at], wd[:, lanes], preferred_element_type=jnp.float32)
        low, high = value[:, :feat], value[:, feat:]
        sib_out[q, at] = jnp.where(core == 0, high, low).astype(jnp.bfloat16)
        send(("sum", q, j), sib_out.at[q, at], sib_in.at[q, at], {"tensor": sib})
        own_part[q, at] = jnp.where(core == 0, low, high)

    def chip_sum(q, s, h):
        if ("sum", q, s // 2) not in summed:
            at = pl.ds(s // 2 * half_rows, half_rows)
            arrive(("sum", q, s // 2), sib_in.at[q, at])
            summed.append(("sum", q, s // 2))
        rows, lanes = slice(s * cap, (s + 1) * cap), slice(h * part, (h + 1) * part)
        return own_part[q, rows, lanes] + sib_in[q, rows, lanes].astype(jnp.float32)

    summed = []

    def sum_d(s, h):
        d_out[s, h] = chip_sum(3, s, h).astype(jnp.bfloat16)
        peer = tx if (s + h) % 2 == 0 else ty
        send(("sd", s, h), d_out.at[s, h], d_in.at[s, h], {"tensor": td if (s, h) in straight_back else peer})

    def diagonal(s, h):
        arrive(("sd", s, h), d_in.at[s, h])
        return d_in[s, h].astype(jnp.float32)

    def sum_x(s, h):
        value = chip_sum(1, s, h)
        if (s + h) % 2 == 1 and (s, h) not in straight_back:
            value = value + diagonal(s, h)
        x_out[s, h] = value.astype(jnp.bfloat16)
        send(("sxy", s, h), x_out.at[s, h], xy_in.at[s, h, 0], {"tensor": tx})

    def sum_y(s, h):
        value = chip_sum(2, s, h)
        if (s + h) % 2 == 0 and (s, h) not in straight_back:
            value = value + diagonal(s, h)
        y_out[s, h] = value.astype(jnp.bfloat16)
        send(("sxy", s, h), y_out.at[s, h], xy_in.at[s, h, 1], {"tensor": ty})

    def total(s, h):
        value = chip_sum(0, s, h)
        if (s, h) in straight_back:
            value = value + diagonal(s, h)
        arrive(("sxy", s, h), xy_in.at[s, h])
        value = value + xy_in[s, h, 0].astype(jnp.float32) + xy_in[s, h, 1].astype(jnp.float32)
        if s == 0:
            z_in[h, rows_of(0)] = value.astype(jnp.bfloat16)
        else:
            z_out[s, h] = value.astype(jnp.bfloat16)
            send("back", z_out.at[s, h], z_in.at[h, rows_of(s)], {"expert": group_of[s]})

    activate(1)
    wait_load(wd_hbm, wd, 2)
    down(3, 1)
    down(1, 1)
    sum_d(2, 0)
    sum_d(2, 1)
    sum_d(3, 0)
    sum_d(3, 1)
    down(2, 1)
    sum_x(2, 0)
    sum_x(3, 1)
    down(0, 1)
    sum_y(2, 1)
    sum_y(3, 0)
    activate(0)
    down(3, 0)
    down(1, 0)
    sum_y(2, 0)
    sum_x(2, 1)
    sum_d(1, 0)
    sum_d(1, 1)
    sum_x(3, 0)
    sum_y(3, 1)
    down(2, 0)
    sum_x(1, 1)
    sum_y(1, 0)
    sum_d(0, 0)
    sum_d(0, 1)
    down(0, 0)
    total(2, 0)
    total(2, 1)
    sum_x(0, 0)
    sum_y(0, 1)
    total(3, 0)
    total(3, 1)
    sum_x(1, 0)
    sum_y(1, 1)
    sum_y(0, 0)
    sum_x(0, 1)
    total(1, 0)
    total(1, 1)
    total(0, 0)
    total(0, 1)

    inputs[2].wait()
    weights = cw_ref[...]
    mixing = match0 * weights[0:1] + match1 * weights[1:2]
    coarse = mixing.astype(jnp.bfloat16)
    fine = (mixing - coarse.astype(jnp.float32)).astype(jnp.bfloat16)
    returned = pl.ds(cap, (groups - 1) * cap)
    arrive("back", z_in.at[:, returned])
    for h in halves:
        combined = contract_first(coarse, z_in[h]) + contract_first(fine, z_in[h])
        out_ref[:, h * part:(h + 1) * part] = combined.astype(jnp.bfloat16)
    total_rows = sum(sent) // wg.shape[1]
    everything = wg.at[pl.ds(0, total_rows)]
    remote("back", everything, everything, {"tensor": sib}).wait_send()


def fused_shards(stashed, expert_ids, combine_weight, w_gate, w_up, w_down):
    groups = lax.axis_size("expert")
    tokens, feat = stashed.shape
    cap = min(tokens, 8 * tokens // (3 * groups))
    _, units, width = w_gate.shape
    rows = groups * cap
    part = feat // 2
    bf16, f32 = jnp.bfloat16, jnp.float32
    hbm = pl.BlockSpec(memory_space=pl.ANY)
    piece = pltpu.VMEM((groups, 2, cap, part), bf16)
    return pl.pallas_call(
        functools.partial(layer_kernel, groups, cap),
        out_shape=pltpu.VMEM((tokens, feat), bf16),
        in_specs=[hbm] * 6,
        out_specs=pl.BlockSpec(memory_space=pltpu.VMEM),
        scratch_shapes=[
            pltpu.VMEM((tokens, feat), bf16),
            pltpu.VMEM((2, tokens), jnp.int32),
            pltpu.VMEM((2, tokens), f32),
            pltpu.VMEM((units, width), bf16),
            pltpu.VMEM((units, width), bf16),
            pltpu.VMEM((units, width), bf16),
            pltpu.VMEM((2, rows - cap, part), bf16),
            pltpu.VMEM((4, 2, 2, rows, part), bf16),
            pltpu.VMEM((rows, units), f32),
            pltpu.VMEM((rows, units), f32),
            pltpu.VMEM((rows, units), bf16),
            pltpu.VMEM((4, rows, feat), bf16),
            pltpu.VMEM((4, rows, feat), bf16),
            pltpu.VMEM((4, rows, feat), f32),
            piece,
            piece,
            piece,
            piece,
            pltpu.VMEM((groups, 2, 2, cap, part), bf16),
            piece,
            pltpu.VMEM((2, rows, part), bf16),
            pltpu.SemaphoreType.DMA((3,)),
            pltpu.SemaphoreType.DMA((3,)),
            pltpu.SemaphoreType.DMA((1,)),
            pltpu.SemaphoreType.DMA((63,)),
        ],
        compiler_params=pltpu.CompilerParams(
            collective_id=0, has_side_effects=True, vmem_limit_bytes=60 * 1024 * 1024
        ),
    )(stashed, expert_ids.T, combine_weight.T, w_gate, w_up, w_down)


def picks_kernel(mesh):
    return mesh.shape["tensor"] == 8 and mesh.shape["expert"] == 4


def solution(mesh):
    return jax.shard_map(
        fused_shards if picks_kernel(mesh) else shards,
        mesh=mesh,
        in_specs=(
            P("expert", "tensor"),
            P("expert", None),
            P("expert", None),
            P("expert", "tensor", None),
            P("expert", "tensor", None),
            P("expert", "tensor", None),
        ),
        out_specs=P("expert", "tensor"),
        check_vma=False,
    )
```

time: 45.1 us -> 39.9 us (0.88)
  Pallas kernels: 43.4 us -> 39.1 us
  local copies, waits for them, and re-layouts: 1.54 us -> 0.64 us
    pallas_call x1, Pallas kernels: 43.4 us -> 39.1 us  [fused_shards(): pl.pallas_call(functools.partial(layer_kernel, groups, cap), out_shape=pl...]
    unnamed x1, local copies, waits for them, and re-layouts: 1.54 us -> 0.64 us
where the time goes in v1:
time: 39.9 us; the launch traced here: 39.7 us
  Pallas kernels  39.1 us (98%)
  local copies, waits for them, and re-layouts  0.64 us (2%)
    pallas_call x1, Pallas kernels, fused_shards(): pl.pallas_call(functools.partial(layer_kernel, groups, cap), out_shape=pl...  39.1 us

profile of v1, /device:TPU:0, one launch (start us, length us, event | category | flops | bytes accessed | tf_op | source)
XLA Modules:
  0.0 39.7 jit_solution(11958077483672492657)
XLA Ops:
  0.0 39.1 %shard_map.64 = bf16[96,512]{1,0:T(8,128)(2,1)S(1)} custom-call(bf16[96,512]{1,0:T(8,128)(2,1)} %x_hbm.1, s32[2,96]{1,0:T(2,128)} %bitcast.2, f32[2,96]{1,0:T(2,128)} %bitcast.3, bf16[1,896,4096]{2,1,0:T(8,128)(2,1)} %wg_hbm.1, bf16[1,896,4096]{2,1,0:T(8,128)(2,1)} %wu_hbm.1, bf16[1,896,4096]{2,1,0:T(8,128)(2,1)} %wd_hbm.1), custom_call_target="tpu_custom_call" | custom-call | tf_op jit(solution)/shard_map/pallas_call | solution.py:393
  39.1 0.6 %copy.8 = bf16[96,512]{1,0:T(8,128)(2,1)} copy(bf16[96,512]{1,0:T(8,128)(2,1)S(1)} %shard_map.64) | data formatting | bytes 196608
